TPU v7x, 32 devices: a whole 2x2x4 slice. The times are simulated.
32 devices in a mesh: beta: 16 (over z, y, x), grp: 2 (over core).
Axes of the slice: x: 2, y: 2, z: 4, core: 2. Of those that a mesh axis runs over, the one named last changes fastest.
Arguments:
- samples: float32 [128, 8, 128, 128], P('beta', 'grp'), parts along dimension 1, may hold values from -6 to 6
Outputs:
- coeffs: float32 [128, 2, 8, 64, 64], P('beta', None, 'grp'), parts along dimension 2
- power: float32 [8, 64], P('grp'), parts along dimension 0
There are 2 independent parts, one for each index of `grp`. A program takes and returns all parts, laid end to end along the dimension named above; each array names one. Nothing has to cross between parts.
All inputs are finite; a program needn't handle non-finite values.
Results may differ from a plain program's by a relative error of at most 0.0003.
Values sent between devices are 32-bit elements; how exact they have to be, the bound alone decides.
No kernel may reach another device: no remote copies, remote signals or barrier semaphores. Data moves between devices by JAX's collectives and lax.ppermute only.
A program may use at most 64 MiB of HBM per device.

v0:
```python
import jax
import jax.numpy as jnp
from jax import lax
from jax.sharding import PartitionSpec as P

HIGHEST = lax.Precision.HIGHEST


def beta_angles(spread):
    grid_size = 2 * spread
    return (2.0 * jnp.arange(grid_size, dtype=jnp.float32) + 1.0) * (jnp.pi / (4.0 * spread))


def quadrature(spread):
    angles = beta_angles(spread)
    odd_terms = 2.0 * jnp.arange(spread, dtype=jnp.float32) + 1.0
    series = jnp.sum(jnp.sin(angles[:, None] * odd_terms[None, :]) / odd_terms[None, :], axis=1)
    return 2.0 / spread * jnp.sin(angles) * series


def gamma_table(spread):
    grid_size = 2 * spread
    positions = jnp.arange(grid_size, dtype=jnp.int32)
    orders = jnp.arange(spread, dtype=jnp.int32)
    phase_index = positions[:, None] * orders[None, :] % grid_size
    angles = phase_index.astype(jnp.float32) * (2.0 * jnp.pi / grid_size)
    return jnp.concatenate([jnp.cos(angles), -jnp.sin(angles)], axis=1)


def alpha_table(spread, row_index):
    grid_size = 2 * spread
    positions = jnp.arange(grid_size, dtype=jnp.int32)
    phase_index = row_index[:, None] * positions[None, :] % grid_size
    angles = phase_index.astype(jnp.float32) * (2.0 * jnp.pi / grid_size)
    cosine = jnp.cos(angles) / grid_size
    sine_part = jnp.sin(angles) / grid_size
    real_rows = jnp.stack([cosine, sine_part], axis=1)
    imag_rows = jnp.stack([-sine_part, cosine], axis=1)
    return jnp.stack([real_rows, imag_rows], axis=0)


def log_factorial(value, float_type):
    return lax.lgamma((value + 1).astype(float_type))


def wigner_start(alpha_order, gamma_order, log_cosine, log_sine):
    float_type = log_cosine.dtype
    lowest = jnp.maximum(jnp.abs(alpha_order), gamma_order)
    shift_low = jnp.maximum(0, gamma_order - alpha_order)
    magnitude = 0.5 * (
        log_factorial(lowest + alpha_order, float_type)
        + log_factorial(lowest - alpha_order, float_type)
        + log_factorial(lowest + gamma_order, float_type)
        + log_factorial(lowest - gamma_order, float_type)
    )
    magnitude = (
        magnitude
        - log_factorial(lowest + gamma_order - shift_low, float_type)
        - log_factorial(shift_low, float_type)
    )
    magnitude = magnitude - log_factorial(alpha_order - gamma_order + shift_low, float_type)
    magnitude = magnitude - log_factorial(lowest - alpha_order - shift_low, float_type)
    cos_power = (2 * lowest + gamma_order - alpha_order - 2 * shift_low).astype(float_type)
    sin_power = (alpha_order - gamma_order + 2 * shift_low).astype(float_type)
    parity = (alpha_order - gamma_order + shift_low) % 2
    sign_factor = (1 - 2 * parity).astype(float_type)
    return sign_factor * jnp.exp(magnitude + cos_power * log_cosine + sin_power * log_sine)


def advance(degree, carried, alpha_order, gamma_order, cos_angles, start_value, lowest):
    former, current = carried
    float_type = current.dtype
    previous = (degree - 1).astype(float_type)
    alpha_float = alpha_order.astype(float_type)
    gamma_float = gamma_order.astype(float_type)
    cross_ratio = alpha_float * gamma_float / jnp.maximum(previous * (previous + 1.0), 1.0)
    upper_term = ((previous + 1.0) * (previous + 1.0) - alpha_float * alpha_float) * (
        (previous + 1.0) * (previous + 1.0) - gamma_float * gamma_float
    )
    lower_term = (previous * previous - alpha_float * alpha_float) * (
        previous * previous - gamma_float * gamma_float
    )
    root_upper = jnp.sqrt(jnp.maximum(upper_term, 1.0))
    forward = (previous + 1.0) * (2.0 * previous + 1.0) / root_upper
    backward = (
        (previous + 1.0)
        * jnp.sqrt(jnp.maximum(lower_term, 0.0))
        / (jnp.maximum(previous, 1.0) * root_upper)
    )
    recurred = forward * (cos_angles - cross_ratio) * current - backward * former
    renewed = jnp.where(degree == lowest, start_value, recurred)
    return (current, renewed)


def degree_rows(row_index, weighted, spread):
    stride = 8
    grid_size = 2 * spread
    group_size = row_index.shape[0]
    channels = weighted.shape[2]
    block_count = spread // stride
    alpha_order = jnp.where(row_index < spread, row_index, row_index - grid_size)[:, None, None]
    gamma_order = jnp.arange(spread, dtype=jnp.int32)[None, None, :]
    angles = beta_angles(spread)
    cos_angles = jnp.cos(angles)[None, :, None]
    log_cosine = jnp.log(jnp.cos(0.5 * angles))[None, :, None]
    log_sine = jnp.log(jnp.sin(0.5 * angles))[None, :, None]
    lowest = jnp.maximum(jnp.abs(alpha_order), gamma_order)
    start_value = wigner_start(alpha_order, gamma_order, log_cosine, log_sine)
    first_block = jnp.min(jnp.abs(alpha_order)) // stride
    empty_state = jnp.zeros((group_size, grid_size, spread), jnp.float32)

    def compute_block(operands):
        block_index, former, current = operands
        levels = []
        for offset in range(stride):
            former, current = advance(
                block_index * stride + offset,
                (former, current),
                alpha_order,
                gamma_order,
                cos_angles,
                start_value,
                lowest,
            )
            levels.append(current)
        stacked = jnp.stack(levels, axis=0)
        block_part = jnp.einsum("jgkq,kgcq->gcjq", stacked, weighted, precision=HIGHEST)
        return (former, current, block_part)

    def skip_block(operands):
        block_index, former, current = operands
        return (former, current, jnp.zeros((group_size, channels, stride, spread), jnp.float32))

    def block_step(carried, block_index):
        former, current = carried
        former, current, block_part = lax.cond(
            block_index >= first_block, compute_block, skip_block, (block_index, former, current)
        )
        return ((former, current), block_part)

    _, parts = lax.scan(
        block_step, (empty_state, empty_state), jnp.arange(block_count, dtype=jnp.int32)
    )
    output = jnp.transpose(parts, (1, 2, 0, 3, 4)).reshape(group_size, channels, spread, spread)
    degree_scale = 8.0 * jnp.sqrt(2.0 * jnp.arange(spread, dtype=jnp.float32) + 1.0)
    return output * degree_scale[None, None, :, None]


def degree_energy(coeffs, functions, spread):
    split_view = coeffs.reshape(coeffs.shape[0], 2, functions, spread, spread)
    multiplicity = jnp.where(jnp.arange(spread) == 0, 1.0, 2.0).astype(jnp.float32)
    energy_sum = jnp.sum(split_view * split_view * multiplicity, axis=(0, 1, 4))
    degrees = 2.0 * jnp.arange(spread, dtype=jnp.float32) + 1.0
    return energy_sum / (degrees * degrees)[None, :]


def local(samples):
    devices = lax.axis_size("beta")
    device = lax.axis_index("beta")
    local_beta = samples.shape[0]
    functions = samples.shape[1]
    grid_size = samples.shape[2]
    spread = grid_size // 2
    channels = 2 * functions
    row_count = grid_size // devices
    natural_rows = jnp.arange(grid_size, dtype=jnp.int32)
    halfway = jnp.einsum("kfag,gx->kfax", samples, gamma_table(spread), precision=HIGHEST)
    halfway = halfway.reshape(local_beta, functions, grid_size, 2, spread)
    spectrum = jnp.einsum(
        "kfacq,spca->kpsfq", halfway, alpha_table(spread, natural_rows), precision=HIGHEST
    )
    spectrum = spectrum.reshape(local_beta, grid_size, channels, spread)
    received = lax.all_to_all(spectrum, "beta", split_axis=1, concat_axis=0, tiled=True)
    weighted = received * quadrature(spread)[:, None, None, None]
    owned_rows = lax.dynamic_slice_in_dim(natural_rows, device * row_count, row_count)
    computed = degree_rows(owned_rows, weighted, spread)
    power_part = degree_energy(computed, functions, spread)
    coeffs = computed
    power = lax.psum(power_part, "beta")
    coeffs = coeffs.reshape(row_count, 2, functions, spread, spread)
    return (coeffs, power)


def solution(mesh):
    return jax.shard_map(
        local,
        mesh=mesh,
        in_specs=(P("beta", "grp", None, None),),
        out_specs=(P("beta", None, "grp", None, None), P("grp", None)),
        check_vma=False,
    )
```

profile of v0, /device:TPU:0, one launch (start us, length us, event | category | flops | bytes accessed | tf_op | source)
XLA Modules:
  0.0 345.6 jit_solution(5608972519271680303)
XLA Ops:
  1.4 0.9 copy-done
  2.2 2.0 fusion.27
  4.2 1.9 convolution_bitcast_fusion.1
  6.1 1.6 copy.57
  7.7 5.6 %copy.58 = f32[8,128,8,64]{3,2,0,1:T(8,128)} copy(f32[8,128,8,64]{1,3,2,0:T(8,128)} %bitcast.233) | data formatting | bytes 4194304 | tf_op jit(solution)/shard_map/reshape | solution.py:172
  13.3 5.5 %reshape.2457 = f32[16,1,32768]{2,1,0:T(1,128)} reshape(f32[128,8,8,64]{3,2,1,0:T(8,128)} %bitcast.230) | data formatting | bytes 4194304
  18.8 8.4 %all-to-all-start = ((f32[16,1,32768]{2,1,0:T(1,128)}), f32[16,1,32768]{2,1,0:T(1,128)}, u32[]{:S(2)}, u32[]{:S(2)}) async-start(f32[16,1,32768]{2,1,0:T(1,128)} %reshape.2457), calls=%async_computation | async-start | bytes 4194304 | tf_op jit(solution)/shard_map/all_to_all | solution.py:173
  27.3 0.7 abs_reduce_fusion
  30.8 0.6 fusion.87
  32.1 38.1 %all-to-all-done = f32[16,1,32768]{2,1,0:T(1,128)} async-done(((f32[16,1,32768]{2,1,0:T(1,128)}), f32[16,1,32768]{2,1,0:T(1,128)}, u32[]{:S(2)}, u32[]{:S(2)}) %all-to-all-start) | async-done | bytes 2097184 | tf_op jit(solution)/shard_map/all_to_all | solution.py:173
  70.3 0.6 broadcast.2681
  70.9 8.6 %reduce.3 = f32[16,32768]{1,0:T(8,128)} reduce(f32[16,1,32768]{2,1,0:T(1,128)} %all-to-all-done, f32[]{:T(128)} %broadcast.2681), dimensions={1}, to_apply=%all_to_all.13.reduce_sub_computation | reduce | bytes 4194308 | tf_op jit(solution)/shard_map/all_to_all | solution.py:173
  79.5 4.2 %reshape.2458 = f32[128,8,8,64]{3,2,1,0:T(8,128)} reshape(f32[16,32768]{1,0:T(8,128)} %reduce.3) | data formatting | bytes 4194304
  83.7 2.8 copy.60
  86.5 2.3 bitcast_multiply_fusion
  88.8 5.0 %copy.61 = f32[128,8,8,64]{0,2,3,1:T(8,128)} copy(f32[128,8,8,64]{3,2,1,0:T(8,128)} %bitcast_multiply_fusion) | data formatting | bytes 4194304
  93.9 182.8 %while.16 = (s32[]{:T(128)}, f32[8,128,64]{1,2,0:T(8,128)S(1)}, f32[8,128,64]{1,2,0:T(8,128)S(1)}, f32[8,8,8,8,64]{2,3,4,1,0:T(8,128)}, s32[8]{0:T(128)S(1)}, /*...) while((s32[]{:T(128)}, f32[8,128,64]{1,2,0:T(8,128)S(1)}, ...), condition=%wide.region_5.6_spmd.clone.clone, body=%wide.region_2.5_spmd.clone.clone.sunk | while | flops 53850804 | bytes 15474387 | solution.py:141
  94.1 0.6 dynamic_slice.13
  95.2 18.6 %conditional.4 = (f32[8,128,64]{1,2,0:T(8,128)S(1)}, f32[8,128,64]{1,2,0:T(8,128)S(1)}, f32[1,8,8,8,64]{2,3,4,1,0:T(8,128)}) conditional(s32[]{:T(128)} %convert_element_type.412, (f32[8,128,64]{1,2,0:T(8,128)S(1)}, f32[8,128,64]{1,2,0:T(8,128)S(1)}) %tuple.139, (s32[]{:T(128)}, s32[8]{0:T(128)S(1)}, s32[8,1,1]{0,2,1:T(1,128)S(1)}, ...), branch_computations={%region_3.3_spmd, %region_4.4_spmd.clone} | conditional | flops 53850800 | bytes 11276004 | solution.py:136
  97.1 3.6 %fusion.11 = (f32[8,128,64]{1,2,0:T(8,128)S(1)}, f32[8,128,64]{1,2,0:T(8,128)S(1)}, f32[8,128,64]{1,2,0:T(8,128)S(1)}, f32[8,128,64]{1,2,0:T(8,128)S(1)}, f32[8,...) fusion(f32[128]{0:T(128)S(1)} %get-tuple-element.437, ...), kind=kLoop, calls=%fused_computation.9 | loop fusion | flops 3473408 | bytes 2684416 | tf_op jit(solution)/shard_map/while/body/eval_jaxpr/cond/branch_1_fun/jit(_where)/select_n | solution.py:91
  100.7 6.2 %stack.51 = f32[8,8,128,64]{2,0,3,1:T(8,128)} concatenate(f32[1,8,128,64]{2,0,3,1:T(1,128)} %bitcast.229, f32[1,8,128,64]{2,0,3,1:T(1,128)} %bitcast.228, f32[1,8,128,64]{2,0,3,1:T(1,128)} %bitcast.227, f32[1,8,128,64]{2,0,3,1:T(1,128)S(1)} %bitcast.226, f32[1,8,128,64]{2,0,3,1:T(1,128)S(1)} %bitcast.225, f32[1,8,128,64]{2,0,3,1:T(1,128)S(1)} %bitcast.224, ...), dimensions={0} | concatenate | bytes 4194304 | tf_op jit(solution)/shard_map/while/body/eval_jaxpr/cond/branch_1_fun/stack | solution.py:126
  106.9 6.9 %convolution_bitcast_fusion = f32[1,8,8,8,64]{2,3,4,1,0:T(8,128)} fusion(f32[8,8,128,64]{2,0,3,1:T(8,128)} %stack.51, f32[128,8,8,64]{0,2,3,1:T(8,128)} %get-tuple-element.428), kind=kOutput, calls=%fused_computation.4 | convolution fusion | flops 50331648 | bytes 4325376 | tf_op jit(solution)/shard_map/while/body/eval_jaxpr/cond/branch_1_fun/jgkq,kgcq->gcjq/dot_general | solution.py:127
  113.8 3.1 constant_dynamic-update-slice_fusion.2
  116.9 0.5 dynamic_slice.13
  118.1 18.6 %conditional.4 = (f32[8,128,64]{1,2,0:T(8,128)S(1)}, f32[8,128,64]{1,2,0:T(8,128)S(1)}, f32[1,8,8,8,64]{2,3,4,1,0:T(8,128)}) conditional(s32[]{:T(128)} %convert_element_type.412, (f32[8,128,64]{1,2,0:T(8,128)S(1)}, f32[8,128,64]{1,2,0:T(8,128)S(1)}) %tuple.139, (s32[]{:T(128)}, s32[8]{0:T(128)S(1)}, s32[8,1,1]{0,2,1:T(1,128)S(1)}, ...), branch_computations={%region_3.3_spmd, %region_4.4_spmd.clone} | conditional | flops 53850800 | bytes 11276004 | solution.py:136
  119.9 3.6 %fusion.11 = (f32[8,128,64]{1,2,0:T(8,128)S(1)}, f32[8,128,64]{1,2,0:T(8,128)S(1)}, f32[8,128,64]{1,2,0:T(8,128)S(1)}, f32[8,128,64]{1,2,0:T(8,128)S(1)}, f32[8,...) fusion(f32[128]{0:T(128)S(1)} %get-tuple-element.437, ...), kind=kLoop, calls=%fused_computation.9 | loop fusion | flops 3473408 | bytes 2684416 | tf_op jit(solution)/shard_map/while/body/eval_jaxpr/cond/branch_1_fun/jit(_where)/select_n | solution.py:91
  123.5 6.2 %stack.51 = f32[8,8,128,64]{2,0,3,1:T(8,128)} concatenate(f32[1,8,128,64]{2,0,3,1:T(1,128)} %bitcast.229, f32[1,8,128,64]{2,0,3,1:T(1,128)} %bitcast.228, f32[1,8,128,64]{2,0,3,1:T(1,128)} %bitcast.227, f32[1,8,128,64]{2,0,3,1:T(1,128)S(1)} %bitcast.226, f32[1,8,128,64]{2,0,3,1:T(1,128)S(1)} %bitcast.225, f32[1,8,128,64]{2,0,3,1:T(1,128)S(1)} %bitcast.224, ...), dimensions={0} | concatenate | bytes 4194304 | tf_op jit(solution)/shard_map/while/body/eval_jaxpr/cond/branch_1_fun/stack | solution.py:126
  129.7 6.9 %convolution_bitcast_fusion = f32[1,8,8,8,64]{2,3,4,1,0:T(8,128)} fusion(f32[8,8,128,64]{2,0,3,1:T(8,128)} %stack.51, f32[128,8,8,64]{0,2,3,1:T(8,128)} %get-tuple-element.428), kind=kOutput, calls=%fused_computation.4 | convolution fusion | flops 50331648 | bytes 4325376 | tf_op jit(solution)/shard_map/while/body/eval_jaxpr/cond/branch_1_fun/jgkq,kgcq->gcjq/dot_general | solution.py:127
  136.7 3.1 constant_dynamic-update-slice_fusion.2
  139.7 0.5 dynamic_slice.13
  140.9 18.6 %conditional.4 = (f32[8,128,64]{1,2,0:T(8,128)S(1)}, f32[8,128,64]{1,2,0:T(8,128)S(1)}, f32[1,8,8,8,64]{2,3,4,1,0:T(8,128)}) conditional(s32[]{:T(128)} %convert_element_type.412, (f32[8,128,64]{1,2,0:T(8,128)S(1)}, f32[8,128,64]{1,2,0:T(8,128)S(1)}) %tuple.139, (s32[]{:T(128)}, s32[8]{0:T(128)S(1)}, s32[8,1,1]{0,2,1:T(1,128)S(1)}, ...), branch_computations={%region_3.3_spmd, %region_4.4_spmd.clone} | conditional | flops 53850800 | bytes 11276004 | solution.py:136
  142.7 3.6 %fusion.11 = (f32[8,128,64]{1,2,0:T(8,128)S(1)}, f32[8,128,64]{1,2,0:T(8,128)S(1)}, f32[8,128,64]{1,2,0:T(8,128)S(1)}, f32[8,128,64]{1,2,0:T(8,128)S(1)}, f32[8,...) fusion(f32[128]{0:T(128)S(1)} %get-tuple-element.437, ...), kind=kLoop, calls=%fused_computation.9 | loop fusion | flops 3473408 | bytes 2684416 | tf_op jit(solution)/shard_map/while/body/eval_jaxpr/cond/branch_1_fun/jit(_where)/select_n | solution.py:91
  146.3 6.2 %stack.51 = f32[8,8,128,64]{2,0,3,1:T(8,128)} concatenate(f32[1,8,128,64]{2,0,3,1:T(1,128)} %bitcast.229, f32[1,8,128,64]{2,0,3,1:T(1,128)} %bitcast.228, f32[1,8,128,64]{2,0,3,1:T(1,128)} %bitcast.227, f32[1,8,128,64]{2,0,3,1:T(1,128)S(1)} %bitcast.226, f32[1,8,128,64]{2,0,3,1:T(1,128)S(1)} %bitcast.225, f32[1,8,128,64]{2,0,3,1:T(1,128)S(1)} %bitcast.224, ...), dimensions={0} | concatenate | bytes 4194304 | tf_op jit(solution)/shard_map/while/body/eval_jaxpr/cond/branch_1_fun/stack | solution.py:126
  152.5 6.9 %convolution_bitcast_fusion = f32[1,8,8,8,64]{2,3,4,1,0:T(8,128)} fusion(f32[8,8,128,64]{2,0,3,1:T(8,128)} %stack.51, f32[128,8,8,64]{0,2,3,1:T(8,128)} %get-tuple-element.428), kind=kOutput, calls=%fused_computation.4 | convolution fusion | flops 50331648 | bytes 4325376 | tf_op jit(solution)/shard_map/while/body/eval_jaxpr/cond/branch_1_fun/jgkq,kgcq->gcjq/dot_general | solution.py:127
  159.5 3.1 constant_dynamic-update-slice_fusion.2
  163.7 18.6 %conditional.4 = (f32[8,128,64]{1,2,0:T(8,128)S(1)}, f32[8,128,64]{1,2,0:T(8,128)S(1)}, f32[1,8,8,8,64]{2,3,4,1,0:T(8,128)}) conditional(s32[]{:T(128)} %convert_element_type.412, (f32[8,128,64]{1,2,0:T(8,128)S(1)}, f32[8,128,64]{1,2,0:T(8,128)S(1)}) %tuple.139, (s32[]{:T(128)}, s32[8]{0:T(128)S(1)}, s32[8,1,1]{0,2,1:T(1,128)S(1)}, ...), branch_computations={%region_3.3_spmd, %region_4.4_spmd.clone} | conditional | flops 53850800 | bytes 11276004 | solution.py:136
  165.5 3.6 %fusion.11 = (f32[8,128,64]{1,2,0:T(8,128)S(1)}, f32[8,128,64]{1,2,0:T(8,128)S(1)}, f32[8,128,64]{1,2,0:T(8,128)S(1)}, f32[8,128,64]{1,2,0:T(8,128)S(1)}, f32[8,...) fusion(f32[128]{0:T(128)S(1)} %get-tuple-element.437, ...), kind=kLoop, calls=%fused_computation.9 | loop fusion | flops 3473408 | bytes 2684416 | tf_op jit(solution)/shard_map/while/body/eval_jaxpr/cond/branch_1_fun/jit(_where)/select_n | solution.py:91
  169.1 6.2 %stack.51 = f32[8,8,128,64]{2,0,3,1:T(8,128)} concatenate(f32[1,8,128,64]{2,0,3,1:T(1,128)} %bitcast.229, f32[1,8,128,64]{2,0,3,1:T(1,128)} %bitcast.228, f32[1,8,128,64]{2,0,3,1:T(1,128)} %bitcast.227, f32[1,8,128,64]{2,0,3,1:T(1,128)S(1)} %bitcast.226, f32[1,8,128,64]{2,0,3,1:T(1,128)S(1)} %bitcast.225, f32[1,8,128,64]{2,0,3,1:T(1,128)S(1)} %bitcast.224, ...), dimensions={0} | concatenate | bytes 4194304 | tf_op jit(solution)/shard_map/while/body/eval_jaxpr/cond/branch_1_fun/stack | solution.py:126
  175.3 6.9 %convolution_bitcast_fusion = f32[1,8,8,8,64]{2,3,4,1,0:T(8,128)} fusion(f32[8,8,128,64]{2,0,3,1:T(8,128)} %stack.51, f32[128,8,8,64]{0,2,3,1:T(8,128)} %get-tuple-element.428), kind=kOutput, calls=%fused_computation.4 | convolution fusion | flops 50331648 | bytes 4325376 | tf_op jit(solution)/shard_map/while/body/eval_jaxpr/cond/branch_1_fun/jgkq,kgcq->gcjq/dot_general | solution.py:127
  182.3 3.1 constant_dynamic-update-slice_fusion.2
  186.5 18.6 %conditional.4 = (f32[8,128,64]{1,2,0:T(8,128)S(1)}, f32[8,128,64]{1,2,0:T(8,128)S(1)}, f32[1,8,8,8,64]{2,3,4,1,0:T(8,128)}) conditional(s32[]{:T(128)} %convert_element_type.412, (f32[8,128,64]{1,2,0:T(8,128)S(1)}, f32[8,128,64]{1,2,0:T(8,128)S(1)}) %tuple.139, (s32[]{:T(128)}, s32[8]{0:T(128)S(1)}, s32[8,1,1]{0,2,1:T(1,128)S(1)}, ...), branch_computations={%region_3.3_spmd, %region_4.4_spmd.clone} | conditional | flops 53850800 | bytes 11276004 | solution.py:136
  188.4 3.6 %fusion.11 = (f32[8,128,64]{1,2,0:T(8,128)S(1)}, f32[8,128,64]{1,2,0:T(8,128)S(1)}, f32[8,128,64]{1,2,0:T(8,128)S(1)}, f32[8,128,64]{1,2,0:T(8,128)S(1)}, f32[8,...) fusion(f32[128]{0:T(128)S(1)} %get-tuple-element.437, ...), kind=kLoop, calls=%fused_computation.9 | loop fusion | flops 3473408 | bytes 2684416 | tf_op jit(solution)/shard_map/while/body/eval_jaxpr/cond/branch_1_fun/jit(_where)/select_n | solution.py:91
  191.9 6.2 %stack.51 = f32[8,8,128,64]{2,0,3,1:T(8,128)} concatenate(f32[1,8,128,64]{2,0,3,1:T(1,128)} %bitcast.229, f32[1,8,128,64]{2,0,3,1:T(1,128)} %bitcast.228, f32[1,8,128,64]{2,0,3,1:T(1,128)} %bitcast.227, f32[1,8,128,64]{2,0,3,1:T(1,128)S(1)} %bitcast.226, f32[1,8,128,64]{2,0,3,1:T(1,128)S(1)} %bitcast.225, f32[1,8,128,64]{2,0,3,1:T(1,128)S(1)} %bitcast.224, ...), dimensions={0} | concatenate | bytes 4194304 | tf_op jit(solution)/shard_map/while/body/eval_jaxpr/cond/branch_1_fun/stack | solution.py:126
  198.2 6.9 %convolution_bitcast_fusion = f32[1,8,8,8,64]{2,3,4,1,0:T(8,128)} fusion(f32[8,8,128,64]{2,0,3,1:T(8,128)} %stack.51, f32[128,8,8,64]{0,2,3,1:T(8,128)} %get-tuple-element.428), kind=kOutput, calls=%fused_computation.4 | convolution fusion | flops 50331648 | bytes 4325376 | tf_op jit(solution)/shard_map/while/body/eval_jaxpr/cond/branch_1_fun/jgkq,kgcq->gcjq/dot_general | solution.py:127
  205.1 3.1 constant_dynamic-update-slice_fusion.2
  209.4 18.6 %conditional.4 = (f32[8,128,64]{1,2,0:T(8,128)S(1)}, f32[8,128,64]{1,2,0:T(8,128)S(1)}, f32[1,8,8,8,64]{2,3,4,1,0:T(8,128)}) conditional(s32[]{:T(128)} %convert_element_type.412, (f32[8,128,64]{1,2,0:T(8,128)S(1)}, f32[8,128,64]{1,2,0:T(8,128)S(1)}) %tuple.139, (s32[]{:T(128)}, s32[8]{0:T(128)S(1)}, s32[8,1,1]{0,2,1:T(1,128)S(1)}, ...), branch_computations={%region_3.3_spmd, %region_4.4_spmd.clone} | conditional | flops 53850800 | bytes 11276004 | solution.py:136
  211.2 3.6 %fusion.11 = (f32[8,128,64]{1,2,0:T(8,128)S(1)}, f32[8,128,64]{1,2,0:T(8,128)S(1)}, f32[8,128,64]{1,2,0:T(8,128)S(1)}, f32[8,128,64]{1,2,0:T(8,128)S(1)}, f32[8,...) fusion(f32[128]{0:T(128)S(1)} %get-tuple-element.437, ...), kind=kLoop, calls=%fused_computation.9 | loop fusion | flops 3473408 | bytes 2684416 | tf_op jit(solution)/shard_map/while/body/eval_jaxpr/cond/branch_1_fun/jit(_where)/select_n | solution.py:91
  214.8 6.2 %stack.51 = f32[8,8,128,64]{2,0,3,1:T(8,128)} concatenate(f32[1,8,128,64]{2,0,3,1:T(1,128)} %bitcast.229, f32[1,8,128,64]{2,0,3,1:T(1,128)} %bitcast.228, f32[1,8,128,64]{2,0,3,1:T(1,128)} %bitcast.227, f32[1,8,128,64]{2,0,3,1:T(1,128)S(1)} %bitcast.226, f32[1,8,128,64]{2,0,3,1:T(1,128)S(1)} %bitcast.225, f32[1,8,128,64]{2,0,3,1:T(1,128)S(1)} %bitcast.224, ...), dimensions={0} | concatenate | bytes 4194304 | tf_op jit(solution)/shard_map/while/body/eval_jaxpr/cond/branch_1_fun/stack | solution.py:126
  221.0 6.9 %convolution_bitcast_fusion = f32[1,8,8,8,64]{2,3,4,1,0:T(8,128)} fusion(f32[8,8,128,64]{2,0,3,1:T(8,128)} %stack.51, f32[128,8,8,64]{0,2,3,1:T(8,128)} %get-tuple-element.428), kind=kOutput, calls=%fused_computation.4 | convolution fusion | flops 50331648 | bytes 4325376 | tf_op jit(solution)/shard_map/while/body/eval_jaxpr/cond/branch_1_fun/jgkq,kgcq->gcjq/dot_general | solution.py:127
  228.0 3.1 constant_dynamic-update-slice_fusion.2
  232.2 18.6 %conditional.4 = (f32[8,128,64]{1,2,0:T(8,128)S(1)}, f32[8,128,64]{1,2,0:T(8,128)S(1)}, f32[1,8,8,8,64]{2,3,4,1,0:T(8,128)}) conditional(s32[]{:T(128)} %convert_element_type.412, (f32[8,128,64]{1,2,0:T(8,128)S(1)}, f32[8,128,64]{1,2,0:T(8,128)S(1)}) %tuple.139, (s32[]{:T(128)}, s32[8]{0:T(128)S(1)}, s32[8,1,1]{0,2,1:T(1,128)S(1)}, ...), branch_computations={%region_3.3_spmd, %region_4.4_spmd.clone} | conditional | flops 53850800 | bytes 11276004 | solution.py:136
  234.0 3.6 %fusion.11 = (f32[8,128,64]{1,2,0:T(8,128)S(1)}, f32[8,128,64]{1,2,0:T(8,128)S(1)}, f32[8,128,64]{1,2,0:T(8,128)S(1)}, f32[8,128,64]{1,2,0:T(8,128)S(1)}, f32[8,...) fusion(f32[128]{0:T(128)S(1)} %get-tuple-element.437, ...), kind=kLoop, calls=%fused_computation.9 | loop fusion | flops 3473408 | bytes 2684416 | tf_op jit(solution)/shard_map/while/body/eval_jaxpr/cond/branch_1_fun/jit(_where)/select_n | solution.py:91
  237.6 6.2 %stack.51 = f32[8,8,128,64]{2,0,3,1:T(8,128)} concatenate(f32[1,8,128,64]{2,0,3,1:T(1,128)} %bitcast.229, f32[1,8,128,64]{2,0,3,1:T(1,128)} %bitcast.228, f32[1,8,128,64]{2,0,3,1:T(1,128)} %bitcast.227, f32[1,8,128,64]{2,0,3,1:T(1,128)S(1)} %bitcast.226, f32[1,8,128,64]{2,0,3,1:T(1,128)S(1)} %bitcast.225, f32[1,8,128,64]{2,0,3,1:T(1,128)S(1)} %bitcast.224, ...), dimensions={0} | concatenate | bytes 4194304 | tf_op jit(solution)/shard_map/while/body/eval_jaxpr/cond/branch_1_fun/stack | solution.py:126
  243.8 6.9 %convolution_bitcast_fusion = f32[1,8,8,8,64]{2,3,4,1,0:T(8,128)} fusion(f32[8,8,128,64]{2,0,3,1:T(8,128)} %stack.51, f32[128,8,8,64]{0,2,3,1:T(8,128)} %get-tuple-element.428), kind=kOutput, calls=%fused_computation.4 | convolution fusion | flops 50331648 | bytes 4325376 | tf_op jit(solution)/shard_map/while/body/eval_jaxpr/cond/branch_1_fun/jgkq,kgcq->gcjq/dot_general | solution.py:127
  250.8 3.1 constant_dynamic-update-slice_fusion.2
  255.0 18.6 %conditional.4 = (f32[8,128,64]{1,2,0:T(8,128)S(1)}, f32[8,128,64]{1,2,0:T(8,128)S(1)}, f32[1,8,8,8,64]{2,3,4,1,0:T(8,128)}) conditional(s32[]{:T(128)} %convert_element_type.412, (f32[8,128,64]{1,2,0:T(8,128)S(1)}, f32[8,128,64]{1,2,0:T(8,128)S(1)}) %tuple.139, (s32[]{:T(128)}, s32[8]{0:T(128)S(1)}, s32[8,1,1]{0,2,1:T(1,128)S(1)}, ...), branch_computations={%region_3.3_spmd, %region_4.4_spmd.clone} | conditional | flops 53850800 | bytes 11276004 | solution.py:136
  256.8 3.6 %fusion.11 = (f32[8,128,64]{1,2,0:T(8,128)S(1)}, f32[8,128,64]{1,2,0:T(8,128)S(1)}, f32[8,128,64]{1,2,0:T(8,128)S(1)}, f32[8,128,64]{1,2,0:T(8,128)S(1)}, f32[8,...) fusion(f32[128]{0:T(128)S(1)} %get-tuple-element.437, ...), kind=kLoop, calls=%fused_computation.9 | loop fusion | flops 3473408 | bytes 2684416 | tf_op jit(solution)/shard_map/while/body/eval_jaxpr/cond/branch_1_fun/jit(_where)/select_n | solution.py:91
  260.4 6.2 %stack.51 = f32[8,8,128,64]{2,0,3,1:T(8,128)} concatenate(f32[1,8,128,64]{2,0,3,1:T(1,128)} %bitcast.229, f32[1,8,128,64]{2,0,3,1:T(1,128)} %bitcast.228, f32[1,8,128,64]{2,0,3,1:T(1,128)} %bitcast.227, f32[1,8,128,64]{2,0,3,1:T(1,128)S(1)} %bitcast.226, f32[1,8,128,64]{2,0,3,1:T(1,128)S(1)} %bitcast.225, f32[1,8,128,64]{2,0,3,1:T(1,128)S(1)} %bitcast.224, ...), dimensions={0} | concatenate | bytes 4194304 | tf_op jit(solution)/shard_map/while/body/eval_jaxpr/cond/branch_1_fun/stack | solution.py:126
  266.7 6.9 %convolution_bitcast_fusion = f32[1,8,8,8,64]{2,3,4,1,0:T(8,128)} fusion(f32[8,8,128,64]{2,0,3,1:T(8,128)} %stack.51, f32[128,8,8,64]{0,2,3,1:T(8,128)} %get-tuple-element.428), kind=kOutput, calls=%fused_computation.4 | convolution fusion | flops 50331648 | bytes 4325376 | tf_op jit(solution)/shard_map/while/body/eval_jaxpr/cond/branch_1_fun/jgkq,kgcq->gcjq/dot_general | solution.py:127
  273.6 3.0 constant_dynamic-update-slice_fusion.2
  276.7 11.1 %copy.62 = f32[8,8,8,8,64]{4,3,2,1,0:T(8,128)} copy(f32[8,8,8,8,64]{1,3,4,0,2:T(8,128)} %bitcast.221) | data formatting | bytes 2097152 | tf_op jit(solution)/shard_map/transpose | solution.py:144
  287.8 8.5 %multiply_reduce_fusion = f32[8,8,8]{0,2,1:T(8,128)S(1)} fusion(f32[64]{0:T(128)S(1)} %compare_select_fusion.9, f32[8,8]{1,0:T(8,128)S(1)} %sqrt_multiply_fusion, f32[8,8,8,8,64]{2,3,4,1,0:T(8,128)} %get-tuple-element.216), kind=kLoop, calls=%fused_computation.97 | loop fusion | flops 1048064 | bytes 1051136 | tf_op jit(solution)/shard_map/reduce_sum | solution.py:152
  296.5 45.8 %psum.7 = f32[4,64]{1,0:T(4,128)} all-reduce(f32[4,64]{1,0:T(4,128)S(1)} %broadcast_divide_fusion), channel_id=1, replica_groups=mesh['beta'=16,'grp'=2] {'beta'}, use_global_device_ids=true, to_apply=%region_8.9 | all-reduce | flops 256 | bytes 2048 | tf_op jit(solution)/shard_map/psum | solution.py:179
  342.3 3.3 broadcast_multiply_fusion
  (264 shorter events, 12.5 us)
Async XLA Ops:
  0.6 1.6 copy-start
  18.8 51.5 %all-to-all-start = ((f32[16,1,32768]{2,1,0:T(1,128)}), f32[16,1,32768]{2,1,0:T(1,128)}, u32[]{:S(2)}, u32[]{:S(2)}) async-start(f32[16,1,32768]{2,1,0:T(1,128)} %reshape.2457), calls=%async_computation | async-start | bytes 4194304 | tf_op jit(solution)/shard_map/all_to_all | solution.py:173
  94.1 1.1 copy-start.2
  113.8 3.1 copy-start.3
  116.9 1.1 copy-start.2
  136.7 3.1 copy-start.3
  139.7 1.1 copy-start.2
  159.5 3.1 copy-start.3
  162.6 1.1 copy-start.2
  182.3 3.1 copy-start.3
  185.4 1.1 copy-start.2
  205.1 3.1 copy-start.3
  208.3 1.1 copy-start.2
  228.0 3.1 copy-start.3
  231.1 1.1 copy-start.2
  250.8 3.1 copy-start.3
  253.9 1.1 copy-start.2
  273.6 3.0 copy-start.3
  287.8 8.7 %copy-start.1 = (f32[64]{0:T(128)S(1)}, f32[64]{0:T(128)}, u32[]{:S(2)}) copy-start(f32[64]{0:T(128)} %fusion.87) | copy-start | bytes 772
where the time goes:
time: 351 us; the launch traced here: 346 us
  local copies, waits for them, and re-layouts  117 us (33%)
  other arithmetic  62.1 us (18%)
  matrix products  59.5 us (17%)
  blocking collectives  45.8 us (13%)
  waiting for transfers between devices  38.1 us (11%)
  loops' own time  11.6 us (3%)
  starting transfers between devices  8.4 us (2%)
  between operations  3.57 us (1%)
    dot_general x8, matrix products, compute_block(): jnp.einsum('jgkq,kgcq->gcjq', stacked, weighted, precision=HIGHEST)  55.6 us
    another operation x8, local copies, waits for them, and re-layouts, compute_block(): stacked = jnp.stack(levels, axis=0)  49.9 us
    psum x1, blocking collectives, local(): power = lax.psum(power_part, 'beta')  45.8 us
    all_to_all x1, waiting for transfers between devices, local(): lax.all_to_all(spectrum, 'beta', split_axis=1, concat_axis=0, tiled=True)  38.1 us
    select_n x8, other arithmetic, advance(): renewed = jnp.where(degree == lowest, start_value, recurred)  28.7 us
    dynamic_update_slice x8, local copies, waits for them, and re-layouts, degree_rows(): lax.scan(block_step, (empty_state, empty_state), jnp.arange(block_count,...  24.7 us
    unnamed x7, local copies, waits for them, and re-layouts  15.6 us
    transpose x1, local copies, waits for them, and re-layouts, degree_rows(): jnp.transpose(parts, (1, 2, 0, 3, 4))  11.1 us
  transfers between devices with their start and end apart: 1, of which 1 were waited for; matrix products, arithmetic and copies ran while one was open for 1% of the time, Pallas kernels for 0%

commit v1 on v0

--- a/solution.py
+++ b/solution.py
@@ -170,7 +170,10 @@
         "kfacq,spca->kpsfq", halfway, alpha_table(spread, natural_rows), precision=HIGHEST
     )
     spectrum = spectrum.reshape(local_beta, grid_size, channels, spread)
-    received = lax.all_to_all(spectrum, "beta", split_axis=1, concat_axis=0, tiled=True)
+    received = jnp.concatenate(
+        lax.all_to_all(jnp.stack(jnp.split(spectrum, lax.axis_size("beta"), axis=1)), "beta", 0, 0),
+        axis=0,
+    )
     weighted = received * quadrature(spread)[:, None, None, None]
     owned_rows = lax.dynamic_slice_in_dim(natural_rows, device * row_count, row_count)
     computed = degree_rows(owned_rows, weighted, spread)

time: 351 us -> 401 us (1.14)
  local copies, waits for them, and re-layouts: 117 us -> 169 us
  matrix products: 59.5 us -> 54.4 us
    another operation x0 -> x18, local copies, waits for them, and re-layouts: none -> 51.8 us  [local(): jnp.stack(jnp.split(spectrum, lax.axis_size('beta'), axis=1))]
    unnamed x7 -> x34, local copies, waits for them, and re-layouts: 15.6 us -> 34.1 us
    another operation x8, local copies, waits for them, and re-layouts: 49.9 us -> 40.8 us  [compute_block(): stacked = jnp.stack(levels, axis=0)]
    reshape x1 -> x0, local copies, waits for them, and re-layouts: 5.57 us -> none  [local(): spectrum = spectrum.reshape(local_beta, grid_size, channels, spread)]
    dot_general x8, matrix products: 55.6 us -> 50.5 us  [compute_block(): jnp.einsum('jgkq,kgcq->gcjq', stacked, weighted, precision=HIGHEST)]
  transfers between devices with their start and end apart: 1 -> 1, of which waited for: 1 -> 1; matrix products, arithmetic and copies ran while one was open for 1% -> 0% of each run, Pallas kernels for 0% -> 0%
where the time goes in v1:
time: 401 us; the launch traced here: 396 us
  local copies, waits for them, and re-layouts  169 us (42%)
  other arithmetic  62.3 us (16%)
  matrix products  54.4 us (14%)
  blocking collectives  45.7 us (11%)
  waiting for transfers between devices  38.9 us (10%)
  loops' own time  14 us (3%)
  starting transfers between devices  8.35 us (2%)
    another operation x18, local copies, waits for them, and re-layouts, local(): jnp.stack(jnp.split(spectrum, lax.axis_size('beta'), axis=1))  51.8 us
    dot_general x8, matrix products, compute_block(): jnp.einsum('jgkq,kgcq->gcjq', stacked, weighted, precision=HIGHEST)  50.5 us
    psum x1, blocking collectives, local(): power = lax.psum(power_part, 'beta')  45.7 us
    another operation x8, local copies, waits for them, and re-layouts, compute_block(): stacked = jnp.stack(levels, axis=0)  40.8 us
    all_to_all x1, waiting for transfers between devices, local(): lax.all_to_all(jnp.stack(jnp.split(spectrum, lax.axis_size('beta'), axis=...  38.9 us
    unnamed x34, local copies, waits for them, and re-layouts  34.1 us
    select_n x8, other arithmetic, advance(): renewed = jnp.where(degree == lowest, start_value, recurred)  28.5 us
    dynamic_update_slice x8, local copies, waits for them, and re-layouts, degree_rows(): lax.scan(block_step, (empty_state, empty_state), jnp.arange(block_count,...  24.6 us
  transfers between devices with their start and end apart: 1, of which 1 were waited for; matrix products, arithmetic and copies ran while one was open for 0% of the time, Pallas kernels for 0%

profile of v1, /device:TPU:0, one launch (start us, length us, event | category | flops | bytes accessed | tf_op | source)
XLA Modules:
  0.0 395.9 jit_solution(16588423047978105721)
XLA Ops:
  6.4 13.4 %slice_bitcast_fusion = (f32[1,8,8,8,64]{2,4,3,1,0:T(8,128)}, f32[1,8,8,8,64]{2,4,3,1,0:T(8,128)}, f32[1,8,8,8,64]{2,4,3,1,0:T(8,128)}, f32[1,8,8,8,64]{2,4,3,1,...) fusion(f32[8,128,8,64]{1,3,2,0:T(8,128)S(1)} %bitcast.248), kind=kLoop, calls=%fused_computation.99 | loop fusion | bytes 4194304 | tf_op jit(solution)/shard_map/stack | solution.py:174
  22.7 3.0 copy.99
  25.7 2.9 copy.100
  28.6 2.9 copy.101
  31.5 2.9 copy.102
  35.7 3.0 copy.104
  38.7 2.9 copy.105
  41.6 2.9 copy.106
  44.5 2.9 copy.107
  48.7 2.3 copy.109
  51.0 2.2 copy.110
  53.2 2.2 copy.111
  76.6 5.5 %reshape.2461 = f32[16,1,32768]{2,1,0:T(1,128)} reshape(f32[16,8,8,8,64]{4,3,2,1,0:T(8,128)} %constant_dynamic-update-slice_fusion.1) | data formatting | bytes 4194304
  82.1 8.3 %all-to-all-start = ((f32[16,1,32768]{2,1,0:T(1,128)}), f32[16,1,32768]{2,1,0:T(1,128)S(1)}, u32[]{:S(2)}, u32[]{:S(2)}) async-start(f32[16,1,32768]{2,1,0:T(1,128)} %reshape.2461), calls=%async_computation | async-start | bytes 4194304 | tf_op jit(solution)/shard_map/all_to_all | solution.py:174
  94.6 38.9 %all-to-all-done = f32[16,1,32768]{2,1,0:T(1,128)S(1)} async-done(((f32[16,1,32768]{2,1,0:T(1,128)}), f32[16,1,32768]{2,1,0:T(1,128)S(1)}, u32[]{:S(2)}, u32[]{:S(2)}) %all-to-all-start) | async-done | bytes 2097184 | tf_op jit(solution)/shard_map/all_to_all | solution.py:174
  135.4 7.3 %reduce.3 = f32[16,32768]{1,0:T(8,128)S(1)} reduce(f32[16,1,32768]{2,1,0:T(1,128)} %copy-done.5, f32[]{:T(128)} %broadcast.2681), dimensions={1}, to_apply=%all_to_all.3.reduce_sub_computation | reduce | bytes 4194308 | tf_op jit(solution)/shard_map/all_to_all | solution.py:174
  142.6 3.0 reshape.2462
  145.6 4.5 %bitcast_multiply_fusion = f32[128,8,8,64]{3,2,1,0:T(8,128)} fusion(f32[16,8,8,8,64]{4,3,2,1,0:T(8,128)} %reshape.2462, f32[128]{0:T(128)S(1)} %multiply_multiply_fusion), kind=kLoop, calls=%fused_computation.98 | loop fusion | flops 524288 | bytes 4194816 | tf_op jit(solution)/shard_map/mul | solution.py:177
  150.2 5.0 %copy.114 = f32[128,8,8,64]{0,2,3,1:T(8,128)} copy(f32[128,8,8,64]{3,2,1,0:T(8,128)} %bitcast_multiply_fusion) | data formatting | bytes 4194304
  155.2 171.6 %while.16 = (s32[]{:T(128)}, f32[8,128,64]{1,2,0:T(8,128)S(1)}, f32[8,128,64]{1,2,0:T(8,128)S(1)}, f32[8,8,8,8,64]{2,3,4,1,0:T(8,128)}, s32[8]{0:T(128)S(1)}, /*...) while((s32[]{:T(128)}, f32[8,128,64]{1,2,0:T(8,128)S(1)}, ...), condition=%wide.region_5.6_spmd.clone.clone, body=%wide.region_2.5_spmd.clone.clone.sunk | while | flops 53850804 | bytes 15474075 | solution.py:141
  156.9 17.0 %conditional.4 = (f32[8,128,64]{1,2,0:T(8,128)S(1)}, f32[8,128,64]{1,2,0:T(8,128)S(1)}, f32[1,8,8,8,64]{2,3,4,1,0:T(8,128)}) conditional(s32[]{:T(128)} %convert_element_type.412, (f32[8,128,64]{1,2,0:T(8,128)S(1)}, f32[8,128,64]{1,2,0:T(8,128)S(1)}) %tuple.154, (s32[]{:T(128)}, s32[8]{0:T(128)S(1)}, s32[8,1,1]{0,2,1:T(1,128)S(1)}, ...), branch_computations={%region_3.3_spmd, %region_4.4_spmd.clone} | conditional | flops 53850800 | bytes 11276004 | solution.py:136
  158.9 3.6 fusion.11
  162.4 5.1 %stack.119 = f32[8,8,128,64]{2,0,3,1:T(8,128)S(1)} concatenate(f32[1,8,128,64]{2,0,3,1:T(1,128)} %bitcast.257, f32[1,8,128,64]{2,0,3,1:T(1,128)} %bitcast.256, f32[1,8,128,64]{2,0,3,1:T(1,128)} %bitcast.255, f32[1,8,128,64]{2,0,3,1:T(1,128)S(1)} %bitcast.254, f32[1,8,128,64]{2,0,3,1:T(1,128)S(1)} %bitcast.253, f32[1,8,128,64]{2,0,3,1:T(1,128)S(1)} %bitcast.252, ...), dimensions={0} | concatenate | bytes 4194304 | tf_op jit(solution)/shard_map/while/body/eval_jaxpr/cond/branch_1_fun/stack | solution.py:126
  167.5 6.3 %convolution_bitcast_fusion = f32[1,8,8,8,64]{2,3,4,1,0:T(8,128)} fusion(f32[8,8,128,64]{2,0,3,1:T(8,128)S(1)} %stack.119, f32[128,8,8,64]{0,2,3,1:T(8,128)} %get-tuple-element.428), kind=kOutput, calls=%fused_computation.4 | convolution fusion | flops 50331648 | bytes 4325376 | tf_op jit(solution)/shard_map/while/body/eval_jaxpr/cond/branch_1_fun/jgkq,kgcq->gcjq/dot_general | solution.py:127
  173.8 3.1 constant_dynamic-update-slice_fusion.18
  178.3 17.0 %conditional.4 = (f32[8,128,64]{1,2,0:T(8,128)S(1)}, f32[8,128,64]{1,2,0:T(8,128)S(1)}, f32[1,8,8,8,64]{2,3,4,1,0:T(8,128)}) conditional(s32[]{:T(128)} %convert_element_type.412, (f32[8,128,64]{1,2,0:T(8,128)S(1)}, f32[8,128,64]{1,2,0:T(8,128)S(1)}) %tuple.154, (s32[]{:T(128)}, s32[8]{0:T(128)S(1)}, s32[8,1,1]{0,2,1:T(1,128)S(1)}, ...), branch_computations={%region_3.3_spmd, %region_4.4_spmd.clone} | conditional | flops 53850800 | bytes 11276004 | solution.py:136
  180.3 3.6 fusion.11
  183.8 5.1 %stack.119 = f32[8,8,128,64]{2,0,3,1:T(8,128)S(1)} concatenate(f32[1,8,128,64]{2,0,3,1:T(1,128)} %bitcast.257, f32[1,8,128,64]{2,0,3,1:T(1,128)} %bitcast.256, f32[1,8,128,64]{2,0,3,1:T(1,128)} %bitcast.255, f32[1,8,128,64]{2,0,3,1:T(1,128)S(1)} %bitcast.254, f32[1,8,128,64]{2,0,3,1:T(1,128)S(1)} %bitcast.253, f32[1,8,128,64]{2,0,3,1:T(1,128)S(1)} %bitcast.252, ...), dimensions={0} | concatenate | bytes 4194304 | tf_op jit(solution)/shard_map/while/body/eval_jaxpr/cond/branch_1_fun/stack | solution.py:126
  188.9 6.3 %convolution_bitcast_fusion = f32[1,8,8,8,64]{2,3,4,1,0:T(8,128)} fusion(f32[8,8,128,64]{2,0,3,1:T(8,128)S(1)} %stack.119, f32[128,8,8,64]{0,2,3,1:T(8,128)} %get-tuple-element.428), kind=kOutput, calls=%fused_computation.4 | convolution fusion | flops 50331648 | bytes 4325376 | tf_op jit(solution)/shard_map/while/body/eval_jaxpr/cond/branch_1_fun/jgkq,kgcq->gcjq/dot_general | solution.py:127
  195.2 3.0 constant_dynamic-update-slice_fusion.18
  199.7 17.0 %conditional.4 = (f32[8,128,64]{1,2,0:T(8,128)S(1)}, f32[8,128,64]{1,2,0:T(8,128)S(1)}, f32[1,8,8,8,64]{2,3,4,1,0:T(8,128)}) conditional(s32[]{:T(128)} %convert_element_type.412, (f32[8,128,64]{1,2,0:T(8,128)S(1)}, f32[8,128,64]{1,2,0:T(8,128)S(1)}) %tuple.154, (s32[]{:T(128)}, s32[8]{0:T(128)S(1)}, s32[8,1,1]{0,2,1:T(1,128)S(1)}, ...), branch_computations={%region_3.3_spmd, %region_4.4_spmd.clone} | conditional | flops 53850800 | bytes 11276004 | solution.py:136
  201.6 3.6 fusion.11
  205.2 5.1 %stack.119 = f32[8,8,128,64]{2,0,3,1:T(8,128)S(1)} concatenate(f32[1,8,128,64]{2,0,3,1:T(1,128)} %bitcast.257, f32[1,8,128,64]{2,0,3,1:T(1,128)} %bitcast.256, f32[1,8,128,64]{2,0,3,1:T(1,128)} %bitcast.255, f32[1,8,128,64]{2,0,3,1:T(1,128)S(1)} %bitcast.254, f32[1,8,128,64]{2,0,3,1:T(1,128)S(1)} %bitcast.253, f32[1,8,128,64]{2,0,3,1:T(1,128)S(1)} %bitcast.252, ...), dimensions={0} | concatenate | bytes 4194304 | tf_op jit(solution)/shard_map/while/body/eval_jaxpr/cond/branch_1_fun/stack | solution.py:126
  210.3 6.3 %convolution_bitcast_fusion = f32[1,8,8,8,64]{2,3,4,1,0:T(8,128)} fusion(f32[8,8,128,64]{2,0,3,1:T(8,128)S(1)} %stack.119, f32[128,8,8,64]{0,2,3,1:T(8,128)} %get-tuple-element.428), kind=kOutput, calls=%fused_computation.4 | convolution fusion | flops 50331648 | bytes 4325376 | tf_op jit(solution)/shard_map/while/body/eval_jaxpr/cond/branch_1_fun/jgkq,kgcq->gcjq/dot_general | solution.py:127
  216.6 3.1 constant_dynamic-update-slice_fusion.18
  221.1 17.0 %conditional.4 = (f32[8,128,64]{1,2,0:T(8,128)S(1)}, f32[8,128,64]{1,2,0:T(8,128)S(1)}, f32[1,8,8,8,64]{2,3,4,1,0:T(8,128)}) conditional(s32[]{:T(128)} %convert_element_type.412, (f32[8,128,64]{1,2,0:T(8,128)S(1)}, f32[8,128,64]{1,2,0:T(8,128)S(1)}) %tuple.154, (s32[]{:T(128)}, s32[8]{0:T(128)S(1)}, s32[8,1,1]{0,2,1:T(1,128)S(1)}, ...), branch_computations={%region_3.3_spmd, %region_4.4_spmd.clone} | conditional | flops 53850800 | bytes 11276004 | solution.py:136
  223.1 3.6 fusion.11
  226.6 5.1 %stack.119 = f32[8,8,128,64]{2,0,3,1:T(8,128)S(1)} concatenate(f32[1,8,128,64]{2,0,3,1:T(1,128)} %bitcast.257, f32[1,8,128,64]{2,0,3,1:T(1,128)} %bitcast.256, f32[1,8,128,64]{2,0,3,1:T(1,128)} %bitcast.255, f32[1,8,128,64]{2,0,3,1:T(1,128)S(1)} %bitcast.254, f32[1,8,128,64]{2,0,3,1:T(1,128)S(1)} %bitcast.253, f32[1,8,128,64]{2,0,3,1:T(1,128)S(1)} %bitcast.252, ...), dimensions={0} | concatenate | bytes 4194304 | tf_op jit(solution)/shard_map/while/body/eval_jaxpr/cond/branch_1_fun/stack | solution.py:126
  231.7 6.3 %convolution_bitcast_fusion = f32[1,8,8,8,64]{2,3,4,1,0:T(8,128)} fusion(f32[8,8,128,64]{2,0,3,1:T(8,128)S(1)} %stack.119, f32[128,8,8,64]{0,2,3,1:T(8,128)} %get-tuple-element.428), kind=kOutput, calls=%fused_computation.4 | convolution fusion | flops 50331648 | bytes 4325376 | tf_op jit(solution)/shard_map/while/body/eval_jaxpr/cond/branch_1_fun/jgkq,kgcq->gcjq/dot_general | solution.py:127
  238.0 3.1 constant_dynamic-update-slice_fusion.18
  242.5 17.0 %conditional.4 = (f32[8,128,64]{1,2,0:T(8,128)S(1)}, f32[8,128,64]{1,2,0:T(8,128)S(1)}, f32[1,8,8,8,64]{2,3,4,1,0:T(8,128)}) conditional(s32[]{:T(128)} %convert_element_type.412, (f32[8,128,64]{1,2,0:T(8,128)S(1)}, f32[8,128,64]{1,2,0:T(8,128)S(1)}) %tuple.154, (s32[]{:T(128)}, s32[8]{0:T(128)S(1)}, s32[8,1,1]{0,2,1:T(1,128)S(1)}, ...), branch_computations={%region_3.3_spmd, %region_4.4_spmd.clone} | conditional | flops 53850800 | bytes 11276004 | solution.py:136
  244.5 3.6 fusion.11
  248.1 5.1 %stack.119 = f32[8,8,128,64]{2,0,3,1:T(8,128)S(1)} concatenate(f32[1,8,128,64]{2,0,3,1:T(1,128)} %bitcast.257, f32[1,8,128,64]{2,0,3,1:T(1,128)} %bitcast.256, f32[1,8,128,64]{2,0,3,1:T(1,128)} %bitcast.255, f32[1,8,128,64]{2,0,3,1:T(1,128)S(1)} %bitcast.254, f32[1,8,128,64]{2,0,3,1:T(1,128)S(1)} %bitcast.253, f32[1,8,128,64]{2,0,3,1:T(1,128)S(1)} %bitcast.252, ...), dimensions={0} | concatenate | bytes 4194304 | tf_op jit(solution)/shard_map/while/body/eval_jaxpr/cond/branch_1_fun/stack | solution.py:126
  253.2 6.3 %convolution_bitcast_fusion = f32[1,8,8,8,64]{2,3,4,1,0:T(8,128)} fusion(f32[8,8,128,64]{2,0,3,1:T(8,128)S(1)} %stack.119, f32[128,8,8,64]{0,2,3,1:T(8,128)} %get-tuple-element.428), kind=kOutput, calls=%fused_computation.4 | convolution fusion | flops 50331648 | bytes 4325376 | tf_op jit(solution)/shard_map/while/body/eval_jaxpr/cond/branch_1_fun/jgkq,kgcq->gcjq/dot_general | solution.py:127
  259.5 3.1 constant_dynamic-update-slice_fusion.18
  264.0 17.0 %conditional.4 = (f32[8,128,64]{1,2,0:T(8,128)S(1)}, f32[8,128,64]{1,2,0:T(8,128)S(1)}, f32[1,8,8,8,64]{2,3,4,1,0:T(8,128)}) conditional(s32[]{:T(128)} %convert_element_type.412, (f32[8,128,64]{1,2,0:T(8,128)S(1)}, f32[8,128,64]{1,2,0:T(8,128)S(1)}) %tuple.154, (s32[]{:T(128)}, s32[8]{0:T(128)S(1)}, s32[8,1,1]{0,2,1:T(1,128)S(1)}, ...), branch_computations={%region_3.3_spmd, %region_4.4_spmd.clone} | conditional | flops 53850800 | bytes 11276004 | solution.py:136
  266.0 3.6 fusion.11
  269.5 5.1 %stack.119 = f32[8,8,128,64]{2,0,3,1:T(8,128)S(1)} concatenate(f32[1,8,128,64]{2,0,3,1:T(1,128)} %bitcast.257, f32[1,8,128,64]{2,0,3,1:T(1,128)} %bitcast.256, f32[1,8,128,64]{2,0,3,1:T(1,128)} %bitcast.255, f32[1,8,128,64]{2,0,3,1:T(1,128)S(1)} %bitcast.254, f32[1,8,128,64]{2,0,3,1:T(1,128)S(1)} %bitcast.253, f32[1,8,128,64]{2,0,3,1:T(1,128)S(1)} %bitcast.252, ...), dimensions={0} | concatenate | bytes 4194304 | tf_op jit(solution)/shard_map/while/body/eval_jaxpr/cond/branch_1_fun/stack | solution.py:126
  274.6 6.3 %convolution_bitcast_fusion = f32[1,8,8,8,64]{2,3,4,1,0:T(8,128)} fusion(f32[8,8,128,64]{2,0,3,1:T(8,128)S(1)} %stack.119, f32[128,8,8,64]{0,2,3,1:T(8,128)} %get-tuple-element.428), kind=kOutput, calls=%fused_computation.4 | convolution fusion | flops 50331648 | bytes 4325376 | tf_op jit(solution)/shard_map/while/body/eval_jaxpr/cond/branch_1_fun/jgkq,kgcq->gcjq/dot_general | solution.py:127
  281.0 3.1 constant_dynamic-update-slice_fusion.18
  285.4 17.0 %conditional.4 = (f32[8,128,64]{1,2,0:T(8,128)S(1)}, f32[8,128,64]{1,2,0:T(8,128)S(1)}, f32[1,8,8,8,64]{2,3,4,1,0:T(8,128)}) conditional(s32[]{:T(128)} %convert_element_type.412, (f32[8,128,64]{1,2,0:T(8,128)S(1)}, f32[8,128,64]{1,2,0:T(8,128)S(1)}) %tuple.154, (s32[]{:T(128)}, s32[8]{0:T(128)S(1)}, s32[8,1,1]{0,2,1:T(1,128)S(1)}, ...), branch_computations={%region_3.3_spmd, %region_4.4_spmd.clone} | conditional | flops 53850800 | bytes 11276004 | solution.py:136
  287.4 3.6 fusion.11
  291.0 5.1 %stack.119 = f32[8,8,128,64]{2,0,3,1:T(8,128)S(1)} concatenate(f32[1,8,128,64]{2,0,3,1:T(1,128)} %bitcast.257, f32[1,8,128,64]{2,0,3,1:T(1,128)} %bitcast.256, f32[1,8,128,64]{2,0,3,1:T(1,128)} %bitcast.255, f32[1,8,128,64]{2,0,3,1:T(1,128)S(1)} %bitcast.254, f32[1,8,128,64]{2,0,3,1:T(1,128)S(1)} %bitcast.253, f32[1,8,128,64]{2,0,3,1:T(1,128)S(1)} %bitcast.252, ...), dimensions={0} | concatenate | bytes 4194304 | tf_op jit(solution)/shard_map/while/body/eval_jaxpr/cond/branch_1_fun/stack | solution.py:126
  296.1 6.3 %convolution_bitcast_fusion = f32[1,8,8,8,64]{2,3,4,1,0:T(8,128)} fusion(f32[8,8,128,64]{2,0,3,1:T(8,128)S(1)} %stack.119, f32[128,8,8,64]{0,2,3,1:T(8,128)} %get-tuple-element.428), kind=kOutput, calls=%fused_computation.4 | convolution fusion | flops 50331648 | bytes 4325376 | tf_op jit(solution)/shard_map/while/body/eval_jaxpr/cond/branch_1_fun/jgkq,kgcq->gcjq/dot_general | solution.py:127
  302.4 3.1 constant_dynamic-update-slice_fusion.18
  306.8 17.0 %conditional.4 = (f32[8,128,64]{1,2,0:T(8,128)S(1)}, f32[8,128,64]{1,2,0:T(8,128)S(1)}, f32[1,8,8,8,64]{2,3,4,1,0:T(8,128)}) conditional(s32[]{:T(128)} %convert_element_type.412, (f32[8,128,64]{1,2,0:T(8,128)S(1)}, f32[8,128,64]{1,2,0:T(8,128)S(1)}) %tuple.154, (s32[]{:T(128)}, s32[8]{0:T(128)S(1)}, s32[8,1,1]{0,2,1:T(1,128)S(1)}, ...), branch_computations={%region_3.3_spmd, %region_4.4_spmd.clone} | conditional | flops 53850800 | bytes 11276004 | solution.py:136
  308.8 3.6 fusion.11
  312.4 5.1 %stack.119 = f32[8,8,128,64]{2,0,3,1:T(8,128)S(1)} concatenate(f32[1,8,128,64]{2,0,3,1:T(1,128)} %bitcast.257, f32[1,8,128,64]{2,0,3,1:T(1,128)} %bitcast.256, f32[1,8,128,64]{2,0,3,1:T(1,128)} %bitcast.255, f32[1,8,128,64]{2,0,3,1:T(1,128)S(1)} %bitcast.254, f32[1,8,128,64]{2,0,3,1:T(1,128)S(1)} %bitcast.253, f32[1,8,128,64]{2,0,3,1:T(1,128)S(1)} %bitcast.252, ...), dimensions={0} | concatenate | bytes 4194304 | tf_op jit(solution)/shard_map/while/body/eval_jaxpr/cond/branch_1_fun/stack | solution.py:126
  317.5 6.3 %convolution_bitcast_fusion = f32[1,8,8,8,64]{2,3,4,1,0:T(8,128)} fusion(f32[8,8,128,64]{2,0,3,1:T(8,128)S(1)} %stack.119, f32[128,8,8,64]{0,2,3,1:T(8,128)} %get-tuple-element.428), kind=kOutput, calls=%fused_computation.4 | convolution fusion | flops 50331648 | bytes 4325376 | tf_op jit(solution)/shard_map/while/body/eval_jaxpr/cond/branch_1_fun/jgkq,kgcq->gcjq/dot_general | solution.py:127
  323.8 3.1 constant_dynamic-update-slice_fusion.18
  326.9 11.1 %copy.115 = f32[8,8,8,8,64]{4,3,2,1,0:T(8,128)} copy(f32[8,8,8,8,64]{1,3,4,0,2:T(8,128)} %bitcast.249) | data formatting | bytes 2097152 | tf_op jit(solution)/shard_map/transpose | solution.py:144
  338.0 8.7 %multiply_reduce_fusion = f32[8,8,8]{0,2,1:T(8,128)S(1)} fusion(f32[64]{0:T(128)S(1)} %compare_select_fusion.9, f32[8,8]{1,0:T(8,128)S(1)} %sqrt_multiply_fusion, f32[8,8,8,8,64]{2,3,4,1,0:T(8,128)} %get-tuple-element.216), kind=kLoop, calls=%fused_computation.97 | loop fusion | flops 1048064 | bytes 1051136 | tf_op jit(solution)/shard_map/reduce_sum | solution.py:152
  346.8 45.7 %psum.7 = f32[4,64]{1,0:T(4,128)} all-reduce(f32[4,64]{1,0:T(4,128)S(1)} %broadcast_divide_fusion), channel_id=1, replica_groups=mesh['beta'=16,'grp'=2] {'beta'}, use_global_device_ids=true, to_apply=%region_8.9 | all-reduce | flops 256 | bytes 2048 | tf_op jit(solution)/shard_map/psum | solution.py:182
  392.6 3.3 broadcast_multiply_fusion
  (275 shorter events, 49.2 us)
Async XLA Ops:
  0.6 1.6 copy-start
  22.7 11.7 %copy-start.4 = (f32[1,8,8,8,64]{2,4,3,1,0:T(8,128)S(1)}, f32[1,8,8,8,64]{2,4,3,1,0:T(8,128)}, u32[]{:S(2)}) copy-start(f32[1,8,8,8,64]{2,4,3,1,0:T(8,128)} %get-tuple-element.583) | copy-start | bytes 393220
  35.7 11.7 %copy-start.3 = (f32[1,8,8,8,64]{2,4,3,1,0:T(8,128)S(1)}, f32[1,8,8,8,64]{2,4,3,1,0:T(8,128)}, u32[]{:S(2)}) copy-start(f32[1,8,8,8,64]{2,4,3,1,0:T(8,128)} %get-tuple-element.578) | copy-start | bytes 393220
  48.7 8.9 %copy-start.2 = (f32[1,8,8,8,64]{2,4,3,1,0:T(8,128)S(1)}, f32[1,8,8,8,64]{2,4,3,1,0:T(8,128)}, u32[]{:S(2)}) copy-start(f32[1,8,8,8,64]{2,4,3,1,0:T(8,128)} %get-tuple-element.573) | copy-start | bytes 393220
  58.2 13.4 %copy-start.7 = (f32[1,8,8,8,64]{4,3,2,1,0:T(8,128)S(1)}, f32[1,8,8,8,64]{4,3,2,1,0:T(8,128)}, u32[]{:S(2)}) copy-start(f32[1,8,8,8,64]{4,3,2,1,0:T(8,128)} %copy.107) | copy-start | bytes 393220
  58.2 14.1 %copy-start.6 = (f32[1,8,8,8,64]{4,3,2,1,0:T(8,128)S(1)}, f32[1,8,8,8,64]{4,3,2,1,0:T(8,128)}, u32[]{:S(2)}) copy-start(f32[1,8,8,8,64]{4,3,2,1,0:T(8,128)} %copy.108) | copy-start | bytes 393220
  82.1 51.4 %all-to-all-start = ((f32[16,1,32768]{2,1,0:T(1,128)}), f32[16,1,32768]{2,1,0:T(1,128)S(1)}, u32[]{:S(2)}, u32[]{:S(2)}) async-start(f32[16,1,32768]{2,1,0:T(1,128)} %reshape.2461), calls=%async_computation | async-start | bytes 4194304 | tf_op jit(solution)/shard_map/all_to_all | solution.py:174
  133.5 1.3 copy-start.5
  338.0 57.9 %copy-start.1 = (f32[8,4,128,128]{3,2,1,0:T(8,128)S(1)}, f32[8,4,128,128]{3,2,1,0:T(8,128)}, u32[]{:S(2)}) copy-start(f32[8,4,128,128]{3,2,1,0:T(8,128)} %param.5) | copy-start | bytes 6291460
